TPU v7x, 32 devices: a whole 2x2x4 slice. The times are simulated.
32 devices in a mesh: tm: 8 (over z, y), space: 4 (over x, core).
Axes of the slice: x: 2, y: 2, z: 4, core: 2. Of those that a mesh axis runs over, the one named last changes fastest.
Arguments:
- source: float32 [8, 32, 128, 128], P('tm', 'space'), may hold values from -8 to 8
- conductivity: float32 [32, 128, 128], P('space'), may hold values from 0.5 to 4
Outputs:
- solution: float32 [8, 32, 128, 128], P('tm', 'space')
- final_defect: float32 [8, 32, 128, 128], P('tm', 'space')
All inputs are finite; a program needn't handle non-finite values.
Results may differ from a plain program's by a relative error of at most 0.000034.
Values sent between devices are 32-bit elements; how exact they have to be, the bound alone decides.
A program may use at most 64 MiB of HBM per device.

v0:
```python
import functools

import jax
import jax.numpy as jnp
from jax import lax
from jax.experimental import pallas as pl
from jax.experimental.pallas import tpu as pltpu
from jax.sharding import PartitionSpec as P

NU = 2
NC = 4


OMEGA = 0.8
FINE = (1.0, 1.0, 1.0)
COARSE = (0.25, 0.25, 1.0)


def padded_2(shard, sides, width):
    for axis, dim in sides:
        peers, length = (lax.axis_size(axis), shard.shape[dim])
        up = [(i, (i + 1) % peers) for i in range(peers - 1)]
        down = [(j, i) for i, j in up]
        last = lax.slice_in_dim(shard, length - width, length, axis=dim)
        first = lax.slice_in_dim(shard, 0, width, axis=dim)
        before = lax.ppermute(last, axis, up)
        after = lax.ppermute(first, axis, down)
        shard = jnp.concatenate([before, shard, after], axis=dim)
    return shard


def shifted(shard, axis, by):
    peers = lax.axis_size(axis)
    pairs = [(i, i + by) for i in range(peers) if 0 <= i + by < peers]
    return lax.ppermute(shard, axis, pairs)


def swapped(value, axis, bit):
    mask = 2**bit
    pairs = [(source, source ^ mask) for source in range(lax.axis_size(axis))]
    return lax.ppermute(value, axis, pairs)


def stencil(padded, weights):
    weight_z, weight_x, weight_y = weights
    centre = padded[1:-1, :, 1:-1]
    widened = jnp.pad(padded[1:-1], ((0, 0), (1, 1), (0, 0)))
    along_z = 2.0 * centre - padded[2:, :, 1:-1] - padded[:-2, :, 1:-1]
    along_x = 2.0 * centre - widened[:, 2:, 1:-1] - widened[:, :-2, 1:-1]
    along_y = 2.0 * centre - padded[1:-1, :, 2:] - padded[1:-1, :, :-2]
    return weight_z * along_z + weight_x * along_x + weight_y * along_y


def defect(current, right_side, earlier, padded, conduct, stretch, weights):
    applied = current + stretch * conduct * stencil(padded, weights)
    return right_side + earlier - applied


def relaxed(current, right_side, earlier, padded, conduct, stretch, weights):
    weight_sum = 2.0 * (weights[0] + weights[1] + weights[2])
    diagonal = 1.0 + stretch * conduct * weight_sum
    return (
        current
        + OMEGA * defect(current, right_side, earlier, padded, conduct, stretch, weights) / diagonal
    )


def coarsen(values):
    return 0.25 * (
        values[..., 0::2, 0::2, :]
        + values[..., 1::2, 0::2, :]
        + (values[..., 0::2, 1::2, :] + values[..., 1::2, 1::2, :])
    )


def refine(values):
    return jnp.repeat(jnp.repeat(values, 2, axis=-3), 2, axis=-2)


def zero_columns(values):
    return jnp.pad(values, ((0, 0), (0, 0), (1, 1)))


def plane_faces(values):
    return padded_2(values, (("space", 0),), 1)


def coarse_planes_framed(values):
    return padded_2(values, (("space", 0),), 1)


def fine_frame(values):
    return zero_columns(plane_faces(values))


def step_prior(values):
    return shifted(values, "tm", 1)


def pair_prior(values):
    return shifted(values, "tm", 2)


def group_prior(values):
    return shifted(values, "tm", 4)


def smooth(current, right_side, conduct, stretch, weights, repeats, earlier_of, framing):
    for turn_index in range(repeats):
        current = relaxed(
            current, right_side, earlier_of(current), framing(current), conduct, stretch, weights
        )
    return current


def body(source, conductivity):
    right_side = source[0]
    solution = smooth(
        jnp.zeros_like(right_side), right_side, conductivity, 1.0, FINE, NU, step_prior, fine_frame
    )
    defect_fine = defect(
        solution, right_side, step_prior(solution), fine_frame(solution), conductivity, 1.0, FINE
    )
    middle_full = defect_fine + swapped(defect_fine, "tm", 0)
    middle = smooth(
        jnp.zeros_like(middle_full),
        middle_full,
        conductivity,
        2.0,
        FINE,
        NU,
        pair_prior,
        fine_frame,
    )
    middle_defect = defect(
        middle, middle_full, pair_prior(middle), fine_frame(middle), conductivity, 2.0, FINE
    )
    summed = middle_defect + swapped(middle_defect, "tm", 1)
    coarse_rhs = coarsen(summed)
    coarse_cond = coarsen(conductivity)

    def coarse_frame(values):
        return zero_columns(coarse_planes_framed(values))

    coarse = smooth(
        jnp.zeros_like(coarse_rhs),
        coarse_rhs,
        coarse_cond,
        4.0,
        COARSE,
        NC,
        group_prior,
        coarse_frame,
    )
    middle = middle + refine(coarse)
    middle = smooth(middle, middle_full, conductivity, 2.0, FINE, NU, pair_prior, fine_frame)
    solution = solution + middle
    solution = smooth(solution, right_side, conductivity, 1.0, FINE, NU, step_prior, fine_frame)
    final_defect = defect(
        solution, right_side, step_prior(solution), fine_frame(solution), conductivity, 1.0, FINE
    )
    return (solution[None], final_defect[None])


MESH = pl.DeviceIdType.MESH


def snake(index):
    return index + ((index // 2) % 2) * (1 - 2 * (index % 2))


def scaled(weights, stretch):
    return tuple(stretch * weight for weight in weights)


def fits(steps, peers, slabs, planes, rows, lanes):
    block = rows // peers
    return (
        steps == peers
        and peers % 8 == 0
        and peers & (peers - 1) == 0
        and rows % peers == 0
        and block % 8 == 0
        and planes % 2 == 0
        and planes >= 6
        and lanes % 128 == 0
        and peers <= 16
        and slabs > 1
    )


PAD, PAD2 = 2, 3


def cycle_kernel(
    peers,
    slabs,
    source_far,
    conduct_far,
    out_solution,
    out_defect,
    rhs, rhs1, rhs2, scrap,
    cond, cond2, gain0, gain1, gain2,
    a1, a2, a3, a4, a5, fd,
    m1, m2, m3, m4,
    k1, k2, k3, k4,
    source, tall,
    in_send, in_recv, own_sem, load_sem,
    tall_send, tall_recv,
    h_send, h_recv,
    out_send, out_recv, out_own,
):
    planes, rows, lanes = source.shape
    block = rows // peers
    half_planes, half_block = planes // 2, block // 2
    reach = 2 * PAD2
    me, slab = lax.axis_index("tm"), lax.axis_index("space")
    mine = snake(me)
    following, preceding = snake((mine + 1) % peers), snake((mine + peers - 1) % peers)
    has_z = {1: slab < slabs - 1, -1: slab > 0, 0: None}
    has_x = {1: mine < peers - 1, -1: mine > 0, 0: None}
    beside = {1: following, -1: preceding}

    def both(first, second):
        if first is None:
            return second
        return first if second is None else first & second

    def device(dz, dx):
        where = {}
        if dx:
            where["tm"] = beside[dx]
        if dz:
            where["space"] = slab + dz
        return where

    def size_of(ref):
        pad = PAD2 if ref.shape[0] == half_planes + 2 * PAD2 else PAD
        return pad, ref.shape[0] - 2 * pad, ref.shape[1] - 2 * pad

    def box(ref, ring):
        pad, depth, width = size_of(ref)
        return (pad - ring, pad + depth + ring, pad - ring, pad + width + ring)

    def strips(ref, outer, inner):
        z0, z1, x0, x1 = box(ref, outer)
        i0, i1, j0, j1 = box(ref, inner)
        return ((z0, i0, x0, x1), (i1, z1, x0, x1), (i0, i1, x0, j0), (i0, i1, j1, x1))

    def over(boxes, work):
        for z0, z1, x0, x1 in boxes:
            if z1 - z0 <= 2 or x1 - x0 <= 4:
                for z in range(z0, z1):
                    work(z, x0, x1)
                continue

            def step(z, _, x0=x0, x1=x1):
                work(z, x0, x1)
                return 0

            lax.fori_loop(z0, z1, step, 0)

    load_source = pltpu.make_async_copy(source_far, source, load_sem.at[0])
    load_conduct = pltpu.make_async_copy(
        conduct_far, tall.at[pl.ds(reach, planes)], load_sem.at[1]
    )
    load_source.start()
    load_conduct.start()

    for ref in (rhs, rhs1, m3, a3, a5, rhs2):

        def clear(z, x0, x1, ref=ref):
            ref[z, x0:x1] = jnp.zeros((x1 - x0, peers, lanes), jnp.float32)

        over(strips(ref, size_of(ref)[0], 0), clear)

    barrier = pltpu.get_barrier_semaphore()
    for k in range(1, peers):
        pl.semaphore_signal(barrier, inc=1, device_id={"tm": me ^ k}, device_id_type=MESH)
    expected = peers - 1
    for dz in (1, -1):
        for dx in (0, 1, -1):
            here = both(has_z[dz], has_x[dx])

            @pl.when(here)
            def _(dz=dz, dx=dx):
                pl.semaphore_signal(
                    barrier, inc=1, device_id=device(dz, dx), device_id_type=MESH
                )

            expected = expected + jnp.where(here, 1, 0)
    load_source.wait()
    pl.semaphore_wait(barrier, expected)

    def rows_of(index):
        return pl.ds(pl.multiple_of(snake(index) * block, 8), block)

    def inward(peer, step, recv):
        return pltpu.make_async_remote_copy(
            src_ref=source.at[:, rows_of(peer), :],
            dst_ref=rhs.at[pl.ds(PAD, planes), pl.ds(PAD, block), step, :],
            send_sem=in_send.at[peer],
            recv_sem=in_recv.at[recv],
            device_id={"tm": peer},
            device_id_type=MESH,
        )

    order = sorted(range(1, peers), reverse=True)
    for k in order:
        inward(me ^ k, me, me).start()
    own = pltpu.make_async_copy(
        source_far.at[:, rows_of(me), :],
        rhs.at[pl.ds(PAD, planes), pl.ds(PAD, block), me, :],
        own_sem,
    )
    own.start()
    load_conduct.wait()

    def tall_copy(side, dz):
        src = planes if dz > 0 else reach
        dst = 0 if dz > 0 else reach + planes
        return pltpu.make_async_remote_copy(
            src_ref=tall.at[pl.ds(src, reach)],
            dst_ref=tall.at[pl.ds(dst, reach)],
            send_sem=tall_send.at[side],
            recv_sem=tall_recv.at[side],
            device_id={"space": slab + dz},
            device_id_type=MESH,
        )

    for side, dz in ((0, 1), (1, -1)):
        pl.when(has_z[dz])(tall_copy(side, dz).start)
    for side, dz in ((0, 1), (1, -1)):
        pl.when(has_z[-dz])(tall_copy(side, dz).wait_recv)

        @pl.when(jnp.logical_not(has_z[-dz]))
        def _(dz=dz):
            start = 0 if dz > 0 else reach + planes
            tall[start : start + reach] = jnp.zeros((reach, rows, lanes), jnp.float32)

    def inside(z, x, factor):
        plane = slab * (planes // factor) + z
        row = mine * (block // factor) + x
        ok = (plane >= 0) & (plane < slabs * planes // factor)
        ok = ok & (row >= 0) & (row < rows // factor)
        return jnp.where(ok, 1.0, 0.0)

    def fill(z, _):
        for x in range(block + 2 * PAD):
            row = jnp.clip(mine * block + x - PAD, 0, rows - 1)
            value = jnp.broadcast_to(tall[z + reach - PAD, pl.ds(row, 1), :], (peers, lanes))
            mask = inside(z - PAD, x - PAD, 1)
            cond[z, x] = value * mask
            gain0[z, x] = mask * (OMEGA / (1.0 + value * (2.0 * sum(FINE))))
            gain1[z, x] = mask * (OMEGA / (1.0 + value * (4.0 * sum(FINE))))
        return 0

    lax.fori_loop(0, planes + 2 * PAD, fill, 0)

    def fill2(z, _):
        for x in range(half_block + 2 * PAD2):
            row = jnp.clip(mine * block + 2 * (x - PAD2), 0, rows - 2)
            quad = (tall[2 * z, pl.ds(row, 1), :] + tall[2 * z + 1, pl.ds(row, 1), :]) + (
                tall[2 * z, pl.ds(row + 1, 1), :] + tall[2 * z + 1, pl.ds(row + 1, 1), :]
            )
            value = jnp.broadcast_to(0.25 * quad, (peers, lanes))
            mask = inside(z - PAD2, x - PAD2, 2)
            cond2[z, x] = value * mask
            gain2[z, x] = mask * (OMEGA / (1.0 + value * (8.0 * sum(COARSE))))
        return 0

    lax.fori_loop(0, half_planes + 2 * PAD2, fill2, 0)

    time = lax.broadcasted_iota(jnp.int32, (1, peers, lanes), 1)
    lane = lax.broadcasted_iota(jnp.int32, (1, peers, lanes), 2)
    not_first, not_last = lane > 0, lane < lanes - 1

    def prior(value, shift):
        return jnp.where(time >= shift, pltpu.roll(value, shift, 1), 0.0)

    def with_partner(value, shift):
        even = (time // shift) % 2 == 0
        return value + jnp.where(
            even, pltpu.roll(value, peers - shift, 1), pltpu.roll(value, shift, 1)
        )

    def residual(ref, z, x0, x1, right, conductivity, weights, shift):
        weight_z, weight_x, weight_y = weights
        at = slice(x0, x1)
        centre = ref[z, at]
        along_z = ref[z - 1, at] + ref[z + 1, at]
        along_x = ref[z, x0 - 1 : x1 - 1] + ref[z, x0 + 1 : x1 + 1]
        along_y = jnp.where(not_first, pltpu.roll(centre, 1, 2), 0.0) + jnp.where(
            not_last, pltpu.roll(centre, lanes - 1, 2), 0.0
        )
        if weight_z == weight_x == weight_y:
            around = weight_z * (6.0 * centre - (along_z + along_x + along_y))
        else:
            around = (2.0 * (weight_z + weight_x + weight_y)) * centre - (
                weight_z * along_z + weight_x * along_x + weight_y * along_y
            )
        left = right[z, at] + prior(centre, shift) - centre - conductivity[z, at] * around
        return centre, left

    def sweeper(new, old, right, conductivity, gain, weights, shift, base=None):
        def work(z, x0, x1):
            centre, left = residual(old, z, x0, x1, right, conductivity, weights, shift)
            value = centre + gain[z, x0:x1] * left
            new[z, x0:x1] = value if base is None else base[z, x0:x1] + value

        return work

    def starter(new, right, gain):
        def work(z, x0, x1):
            new[z, x0:x1] = gain[z, x0:x1] * right[z, x0:x1]

        return work

    def defecter(new, old, right, weights, shift, pairs):
        def work(z, x0, x1):
            left = residual(old, z, x0, x1, right, cond, weights, shift)[1]
            new[z, x0:x1] = with_partner(left, 1) if pairs else left

        return work

    def wide(ref, depth, corner, stage):
        pad, deep, broad = size_of(ref)

        def spans(step, size, count):
            if step == 0:
                return pl.ds(pad, size), pl.ds(pad, size)
            if step > 0:
                return pl.ds(pad + size - count, count), pl.ds(pad - count, count)
            return pl.ds(pad, count), pl.ds(pad + size, count)

        out = []
        steps = [(dz, dx) for dz in (1, -1) for dx in (1, -1)] if corner else []
        for number, (dz, dx) in enumerate(steps + [(0, 1), (0, -1), (1, 0), (-1, 0)]):
            count = corner if dz and dx else depth
            src_z, dst_z = spans(dz, deep, count)
            src_x, dst_x = spans(dx, broad, count)
            copy = pltpu.make_async_remote_copy(
                src_ref=ref.at[src_z, src_x],
                dst_ref=ref.at[dst_z, dst_x],
                send_sem=h_send.at[stage, number],
                recv_sem=h_recv.at[stage, number],
                device_id=device(dz, dx),
                device_id_type=MESH,
            )
            sends = both(has_z[dz], has_x[dx])
            arrives = both(has_z[-dz], has_x[-dx])
            out.append((sends, arrives, copy))
        return out

    started = []

    def send(ref, depth, corner, stage):
        copies = wide(ref, depth, corner, stage)
        for sends, _, copy in copies:
            pl.when(sends)(copy.start)
        started.append(copies)

    def receive():
        for _, arrives, copy in started[-1]:
            pl.when(arrives)(copy.wait_recv)

    fine, middle, coarse = FINE, scaled(FINE, 2.0), scaled(COARSE, 4.0)

    def pieces_of(ref, edge):
        _, deep, broad = size_of(ref)
        return (
            (edge, deep - 2 * edge, edge, broad - 2 * edge),
            (0, edge, 0, broad),
            (deep - edge, edge, 0, broad),
            (edge, deep - 2 * edge, 0, edge),
            (edge, deep - 2 * edge, broad - edge, edge),
        )

    pieces = [(a5, out_solution, part) for part in pieces_of(a5, 2)]
    pieces.append((fd, out_defect, (0, planes, 0, block)))

    def ends(piece, step, owner):
        src, dst, (z, deep, x, broad) = pieces[piece]
        return (
            src.at[pl.ds(z + PAD, deep), pl.ds(x + PAD, broad), step, :],
            dst.at[pl.ds(z, deep), pl.ds(snake(owner) * block + x, broad), :],
        )

    def outward(piece, peer, owner):
        src, dst = ends(piece, peer, owner)
        return pltpu.make_async_remote_copy(
            src_ref=src,
            dst_ref=dst,
            send_sem=out_send.at[piece, peer],
            recv_sem=out_recv.at[piece, owner],
            device_id={"tm": peer},
            device_id_type=MESH,
        )

    def home(piece):
        src, dst = ends(piece, me, me)
        return pltpu.make_async_copy(src, dst, out_own.at[piece])

    def ship(piece):
        for k in order:
            outward(piece, me ^ k, me).start()
        home(piece).start()

    def stages(boxes_of, works):
        for work, (ref, rings) in zip(works, boxes_of):
            over(strips(ref, *rings) if isinstance(rings, tuple) else (box(ref, rings),), work)

    def presmooth(x, right, one, two, left, gain, weights, shift, pairs):
        works = (
            starter(one, right, gain),
            sweeper(two, one, right, cond, gain, weights, shift),
            defecter(left, two, right, weights, shift, pairs),
        )
        send(right, 2, 1, x)
        stages(((one, 0), (two, -1), (left, -2)), works)
        receive()
        stages(((one, (2, 0)), (two, (1, -1)), (left, (0, -2))), works)

    own.wait()
    for k in order:
        inward(me, me ^ k, me ^ k).wait_recv()
    presmooth(0, rhs, a1, a2, rhs1, gain0, fine, 1, True)
    presmooth(1, rhs1, m1, m2, scrap, gain1, middle, 2, False)

    def restrict(z, _):
        for x in range(half_block):
            zz, xx = 2 * z + PAD, 2 * x + PAD
            quad = (scrap[zz, xx] + scrap[zz + 1, xx]) + (
                scrap[zz, xx + 1] + scrap[zz + 1, xx + 1]
            )
            rhs2[z + PAD2, x + PAD2] = 0.25 * with_partner(quad[None], 2)[0]
        return 0

    lax.fori_loop(0, half_planes, restrict, 0)
    send(rhs2, 3, 2, 2)
    start = starter(k1, rhs2, gain2)
    works = [
        sweeper(new, old, rhs2, cond2, gain2, coarse, 4)
        for new, old in ((k2, k1), (k3, k2), (k4, k3))
    ]
    stages(((k1, 0), (k2, -1)), (start, works[0]))
    receive()
    stages(((k1, (3, 0)), (k2, (2, -1)), (k3, 1), (k4, 0)), (start, *works))

    def prolong(z, x0, x1):
        for x in range(x0, x1):
            value = k4[z, x]
            for dz in range(2):
                for dx in range(2):
                    at = (2 * (z - PAD2) + dz + PAD, 2 * (x - PAD2) + dx + PAD)
                    m3[at] = m2[at] + value

    over(strips(k4, 0, -1), prolong)
    send(m3, 2, 1, 3)
    over((box(k4, -1),), prolong)
    works = (
        sweeper(m4, m3, rhs1, cond, gain1, middle, 2),
        sweeper(a3, m4, rhs1, cond, gain1, middle, 2, a2),
    )
    stages(((m4, -1), (a3, -2)), works)
    receive()
    stages(((m4, (1, -1)), (a3, (0, -2))), works)
    send(a3, 2, 1, 4)
    works = (
        sweeper(a4, a3, rhs, cond, gain0, fine, 1),
        sweeper(a5, a4, rhs, cond, gain0, fine, 1),
    )
    stages(((a4, -1), (a5, -2)), works)
    ship(0)
    receive()
    stages(((a4, (1, -1)), (a5, (0, -2))), works)
    send(a5, 1, 0, 5)
    for piece in range(1, 5):
        ship(piece)
    works = (defecter(fd, a5, rhs, fine, 1, False),)
    stages(((fd, -1),), works)
    receive()
    stages(((fd, (0, -1)),), works)
    ship(5)

    for copies in started:
        for sends, _, copy in copies:
            pl.when(sends)(copy.wait_send)
    for side, dz in ((0, 1), (1, -1)):
        pl.when(has_z[dz])(tall_copy(side, dz).wait_send)
    for k in order:
        inward(me ^ k, me, me).wait_send()
    for piece in range(6):
        home(piece).wait()
        for k in order:
            outward(piece, me ^ k, me).wait_send()
            outward(piece, me, me ^ k).wait_recv()


def fused_body(peers, slabs, source, conductivity):
    _, planes, rows, lanes = source.shape
    block = rows // peers

    def field(depth, width):
        return pltpu.VMEM((depth, width, peers, lanes), jnp.float32)

    large = field(planes + 2 * PAD, block + 2 * PAD)
    small = field(planes // 2 + 2 * PAD2, block // 2 + 2 * PAD2)
    dma = pltpu.SemaphoreType.DMA
    anywhere = pl.BlockSpec(memory_space=pl.ANY)
    shape = jax.ShapeDtypeStruct((planes, rows, lanes), jnp.float32)
    solution, final_defect = pl.pallas_call(
        functools.partial(cycle_kernel, peers, slabs),
        out_shape=(shape, shape),
        in_specs=[anywhere, anywhere],
        out_specs=(anywhere, anywhere),
        scratch_shapes=[
            large, large, small, large,
            large, small, large, large, small,
            large, large, large, large, large, large,
            large, large, large, large,
            small, small, small, small,
            pltpu.VMEM((planes, rows, lanes), jnp.float32),
            pltpu.VMEM((planes + 4 * PAD2, rows, lanes), jnp.float32),
            dma((peers,)), dma((peers,)), dma, dma((2,)),
            dma((2,)), dma((2,)),
            dma((6, 8)), dma((6, 8)),
            dma((6, peers)), dma((6, peers)), dma((6,)),
        ],
        compiler_params=pltpu.CompilerParams(
            collective_id=0, has_side_effects=True, vmem_limit_bytes=60 * 1024 * 1024
        ),
    )(source[0], conductivity)
    return (solution[None], final_defect[None])


def solution(mesh):
    peers, slabs = mesh.shape["tm"], mesh.shape["space"]

    def chosen(source, conductivity):
        steps, planes, rows, lanes = source.shape
        if fits(steps * peers, peers, slabs, planes, rows, lanes):
            return fused_body(peers, slabs, source, conductivity)
        return body(source, conductivity)

    return jax.shard_map(
        chosen,
        mesh=mesh,
        in_specs=(P("tm", "space", None, None), P("space", None, None)),
        out_specs=(P("tm", "space", None, None), P("tm", "space", None, None)),
        check_vma=False,
    )
```

profile of v0, /device:TPU:0, one launch (start us, length us, event | category | flops | bytes accessed | tf_op | source)
XLA Modules:
  0.0 69.8 jit_solution(9971952141769391489)
XLA Ops:
  0.6 66.4 %shard_map.41 = (f32[8,128,128]{2,1,0:T(8,128)}, f32[8,128,128]{2,1,0:T(8,128)}) custom-call(f32[8,128,128]{2,1,0:T(8,128)} %bitcast.3, f32[8,128,128]{2,1,0:T(8,128)} %conduct_far.1), custom_call_target="tpu_custom_call" | custom-call | tf_op jit(solution)/shard_map/pallas_call | solution.py:612
  67.0 0.0 copy-start
  67.0 1.9 %copy.6 = f32[1,8,128,128]{3,2,1,0:T(8,128)} copy(f32[1,8,128,128]{3,2,1,0:T(8,128)} %bitcast.5) | data formatting | bytes 1048576
  69.0 0.0 copy-done
  69.0 0.8 %copy.7 = f32[1,8,128,128]{3,2,1,0:T(8,128)} copy(f32[1,8,128,128]{3,2,1,0:T(8,128)S(1)} %bitcast.4) | data formatting | bytes 1048576
Async XLA Ops:
  67.0 1.9 %copy-start = (f32[8,128,128]{2,1,0:T(8,128)S(1)}, f32[8,128,128]{2,1,0:T(8,128)}, u32[]{:S(2)}) copy-start(f32[8,128,128]{2,1,0:T(8,128)} %get-tuple-element.5) | copy-start | bytes 1572868
where the time goes:
time: 69.9 us; the launch traced here: 69.8 us
  Pallas kernels  66.4 us (95%)
  local copies, waits for them, and re-layouts  2.73 us (4%)
    pallas_call x1, Pallas kernels, fused_body(): pl.pallas_call(functools.partial(cycle_kernel, peers, slabs), out_shape=(...  66.4 us
    unnamed x4, local copies, waits for them, and re-layouts  2.73 us

commit v1 on v0

--- a/solution.py
+++ b/solution.py
@@ -182,14 +182,16 @@
         and rows % peers == 0
         and block % 8 == 0
         and planes % 2 == 0
-        and planes >= 6
+        and planes >= 8
         and lanes % 128 == 0
-        and peers <= 16
+        and peers == 8
         and slabs > 1
     )
 
 
-PAD, PAD2 = 2, 3
+PAD, PAD2 = 3, 4
+NEAR = 2 * PAD2
+UNROLL = 24
 
 
 def cycle_kernel(
@@ -200,20 +202,19 @@
     out_solution,
     out_defect,
     rhs, rhs1, rhs2, scrap,
-    cond, cond2, gain0, gain1, gain2,
+    cond, gain0, hold0, gain1, hold1, gain2, hold2,
     a1, a2, a3, a4, a5, fd,
-    m1, m2, m3, m4,
+    m1, m2, m3, m4, m5,
     k1, k2, k3, k4,
-    source, tall,
-    in_send, in_recv, own_sem, load_sem,
-    tall_send, tall_recv,
+    source,
+    in_send, in_recv, own_sem, load_sem, cond_load,
+    cond_send, cond_recv,
     h_send, h_recv,
     out_send, out_recv, out_own,
 ):
     planes, rows, lanes = source.shape
     block = rows // peers
     half_planes, half_block = planes // 2, block // 2
-    reach = 2 * PAD2
     me, slab = lax.axis_index("tm"), lax.axis_index("space")
     mine = snake(me)
     following, preceding = snake((mine + 1) % peers), snake((mine + peers - 1) % peers)
@@ -238,41 +239,49 @@
         pad = PAD2 if ref.shape[0] == half_planes + 2 * PAD2 else PAD
         return pad, ref.shape[0] - 2 * pad, ref.shape[1] - 2 * pad
 
-    def box(ref, ring):
+    def over(ref, outer, inner, work):
         pad, depth, width = size_of(ref)
-        return (pad - ring, pad + depth + ring, pad - ring, pad + width + ring)
-
-    def strips(ref, outer, inner):
-        z0, z1, x0, x1 = box(ref, outer)
-        i0, i1, j0, j1 = box(ref, inner)
-        return ((z0, i0, x0, x1), (i1, z1, x0, x1), (i0, i1, x0, j0), (i0, i1, j1, x1))
-
-    def over(boxes, work):
-        for z0, z1, x0, x1 in boxes:
-            if z1 - z0 <= 2 or x1 - x0 <= 4:
-                for z in range(z0, z1):
-                    work(z, x0, x1)
+        z0, z1, x0, x1 = pad - outer, pad + depth + outer, pad - outer, pad + width + outer
+        parts = []
+        if inner is None:
+            parts.append((z0, z1, list(range(x0, x1))))
+        else:
+            i0, i1, j0, j1 = pad - inner, pad + depth + inner, pad - inner, pad + width + inner
+            parts.append((z0, i0, list(range(x0, x1))))
+            parts.append((i1, z1, list(range(x0, x1))))
+            parts.append((i0, i1, list(range(x0, j0)) + list(range(j1, x1))))
+        for first, last, xs in parts:
+            count = last - first
+            if count <= 0 or not xs:
                 continue
-
-            def step(z, _, x0=x0, x1=x1):
-                work(z, x0, x1)
+            folds = [u for u in range(1, count + 1) if count % u == 0 and u * len(xs) <= UNROLL]
+            fold = max(folds) if folds else 1
+            if fold == count:
+                for z in range(first, last):
+                    work(z, xs)
+                continue
+
+            def step(i, _, first=first, xs=xs, fold=fold):
+                for u in range(fold):
+                    work(first + i * fold + u, xs)
                 return 0
 
-            lax.fori_loop(z0, z1, step, 0)
-
-    load_source = pltpu.make_async_copy(source_far, source, load_sem.at[0])
-    load_conduct = pltpu.make_async_copy(
-        conduct_far, tall.at[pl.ds(reach, planes)], load_sem.at[1]
-    )
+            lax.fori_loop(0, count // fold, step, 0)
+
+    load_source = pltpu.make_async_copy(source_far, source, load_sem)
     load_source.start()
-    load_conduct.start()
-
-    for ref in (rhs, rhs1, m3, a3, a5, rhs2):
-
-        def clear(z, x0, x1, ref=ref):
-            ref[z, x0:x1] = jnp.zeros((x1 - x0, peers, lanes), jnp.float32)
-
-        over(strips(ref, size_of(ref)[0], 0), clear)
+
+    def window(number):
+        start, count, at = ((0, block, NEAR), (-NEAR, NEAR, 0), (block, NEAR, NEAR + block))[number]
+        return pltpu.make_async_copy(
+            conduct_far.at[:, pl.ds(pl.multiple_of(mine * block + start, 8), count), :],
+            cond.at[pl.ds(NEAR, planes), pl.ds(at, count), :],
+            cond_load.at[number],
+        )
+
+    window(0).start()
+    pl.when(has_x[-1])(window(1).start)
+    pl.when(has_x[1])(window(2).start)
 
     barrier = pltpu.get_barrier_semaphore()
     for k in range(1, peers):
@@ -314,116 +323,156 @@
         own_sem,
     )
     own.start()
-    load_conduct.wait()
-
-    def tall_copy(side, dz):
-        src = planes if dz > 0 else reach
-        dst = 0 if dz > 0 else reach + planes
+    window(0).wait()
+    pl.when(has_x[-1])(window(1).wait)
+    pl.when(has_x[1])(window(2).wait)
+
+    def cond_copy(side, dz):
         return pltpu.make_async_remote_copy(
-            src_ref=tall.at[pl.ds(src, reach)],
-            dst_ref=tall.at[pl.ds(dst, reach)],
-            send_sem=tall_send.at[side],
-            recv_sem=tall_recv.at[side],
+            src_ref=cond.at[pl.ds(planes, NEAR) if dz > 0 else pl.ds(NEAR, NEAR)],
+            dst_ref=cond.at[pl.ds(0, NEAR) if dz > 0 else pl.ds(NEAR + planes, NEAR)],
+            send_sem=cond_send.at[side],
+            recv_sem=cond_recv.at[side],
             device_id={"space": slab + dz},
             device_id_type=MESH,
         )
 
     for side, dz in ((0, 1), (1, -1)):
-        pl.when(has_z[dz])(tall_copy(side, dz).start)
+        pl.when(has_z[dz])(cond_copy(side, dz).start)
+
+    for ref in (rhs, rhs1, a3, m3, m5, rhs2):
+        pad, deep, broad = size_of(ref)
+        for dz, first in ((-1, 0), (1, pad + deep)):
+
+            @pl.when(jnp.logical_not(has_z[dz]))
+            def _(ref=ref, first=first, pad=pad):
+                def clear(z, _):
+                    ref[z] = jnp.zeros(ref.shape[1:], jnp.float32)
+                    return 0
+
+                lax.fori_loop(first, first + pad, clear, 0)
+
+        for dx, first in ((-1, 0), (1, pad + broad)):
+
+            @pl.when(jnp.logical_not(has_x[dx]))
+            def _(ref=ref, first=first, pad=pad):
+                def clear(z, _):
+                    ref[z, first : first + pad] = jnp.zeros((pad, peers, lanes), jnp.float32)
+                    return 0
+
+                lax.fori_loop(0, ref.shape[0], clear, 0)
+
     for side, dz in ((0, 1), (1, -1)):
-        pl.when(has_z[-dz])(tall_copy(side, dz).wait_recv)
-
-        @pl.when(jnp.logical_not(has_z[-dz]))
-        def _(dz=dz):
-            start = 0 if dz > 0 else reach + planes
-            tall[start : start + reach] = jnp.zeros((reach, rows, lanes), jnp.float32)
-
-    def inside(z, x, factor):
-        plane = slab * (planes // factor) + z
-        row = mine * (block // factor) + x
-        ok = (plane >= 0) & (plane < slabs * planes // factor)
-        ok = ok & (row >= 0) & (row < rows // factor)
-        return jnp.where(ok, 1.0, 0.0)
+        pl.when(has_z[-dz])(cond_copy(side, dz).wait_recv)
 
     def fill(z, _):
-        for x in range(block + 2 * PAD):
-            row = jnp.clip(mine * block + x - PAD, 0, rows - 1)
-            value = jnp.broadcast_to(tall[z + reach - PAD, pl.ds(row, 1), :], (peers, lanes))
-            mask = inside(z - PAD, x - PAD, 1)
-            cond[z, x] = value * mask
-            gain0[z, x] = mask * (OMEGA / (1.0 + value * (2.0 * sum(FINE))))
-            gain1[z, x] = mask * (OMEGA / (1.0 + value * (4.0 * sum(FINE))))
+        plane = slab * planes + z - PAD
+        deep = (plane >= 0) & (plane < slabs * planes)
+        for part in range((block + 2 * NEAR) // 8):
+            at = pl.ds(8 * part, 8)
+            row = mine * block - NEAR + 8 * part + lax.broadcasted_iota(jnp.int32, (8, lanes), 0)
+            ok = deep & (row >= 0) & (row < rows)
+            value = jnp.where(ok, cond[z - PAD + NEAR, at, :], 0.0)
+            fine = jnp.where(ok, OMEGA / (1.0 + value * (2.0 * sum(FINE))), 0.0)
+            middle = jnp.where(ok, OMEGA / (1.0 + value * (4.0 * sum(FINE))), 0.0)
+            gain0[z, at, :] = fine
+            hold0[z, at, :] = fine * value
+            gain1[z, at, :] = middle
+            hold1[z, at, :] = middle * (2.0 * value)
         return 0
 
     lax.fori_loop(0, planes + 2 * PAD, fill, 0)
 
     def fill2(z, _):
-        for x in range(half_block + 2 * PAD2):
-            row = jnp.clip(mine * block + 2 * (x - PAD2), 0, rows - 2)
-            quad = (tall[2 * z, pl.ds(row, 1), :] + tall[2 * z + 1, pl.ds(row, 1), :]) + (
-                tall[2 * z, pl.ds(row + 1, 1), :] + tall[2 * z + 1, pl.ds(row + 1, 1), :]
+        plane = slab * half_planes + z - PAD2
+        deep = (plane >= 0) & (plane < slabs * half_planes)
+        for part in range((block + 2 * NEAR) // 16):
+            at = pl.ds(8 * part, 8)
+            even, odd = pl.ds(16 * part, 8, stride=2), pl.ds(16 * part + 1, 8, stride=2)
+            quad = (cond[2 * z, even, :] + cond[2 * z + 1, even, :]) + (
+                cond[2 * z, odd, :] + cond[2 * z + 1, odd, :]
             )
-            value = jnp.broadcast_to(0.25 * quad, (peers, lanes))
-            mask = inside(z - PAD2, x - PAD2, 2)
-            cond2[z, x] = value * mask
-            gain2[z, x] = mask * (OMEGA / (1.0 + value * (8.0 * sum(COARSE))))
+            row = mine * half_block - PAD2 + 8 * part
+            row = row + lax.broadcasted_iota(jnp.int32, (8, lanes), 0)
+            ok = deep & (row >= 0) & (row < rows // 2)
+            value = jnp.where(ok, 0.25 * quad, 0.0)
+            gain = jnp.where(ok, OMEGA / (1.0 + value * (8.0 * sum(COARSE))), 0.0)
+            gain2[z, at, :] = gain
+            hold2[z, at, :] = gain * value
         return 0
 
     lax.fori_loop(0, half_planes + 2 * PAD2, fill2, 0)
 
-    time = lax.broadcasted_iota(jnp.int32, (1, peers, lanes), 1)
-    lane = lax.broadcasted_iota(jnp.int32, (1, peers, lanes), 2)
+    time = lax.broadcasted_iota(jnp.int32, (peers, lanes), 0)
+    lane = lax.broadcasted_iota(jnp.int32, (peers, lanes), 1)
     not_first, not_last = lane > 0, lane < lanes - 1
-
-    def prior(value, shift):
-        return jnp.where(time >= shift, pltpu.roll(value, shift, 1), 0.0)
-
-    def with_partner(value, shift):
-        even = (time // shift) % 2 == 0
-        return value + jnp.where(
-            even, pltpu.roll(value, peers - shift, 1), pltpu.roll(value, shift, 1)
-        )
-
-    def residual(ref, z, x0, x1, right, conductivity, weights, shift):
-        weight_z, weight_x, weight_y = weights
-        at = slice(x0, x1)
-        centre = ref[z, at]
-        along_z = ref[z - 1, at] + ref[z + 1, at]
-        along_x = ref[z, x0 - 1 : x1 - 1] + ref[z, x0 + 1 : x1 + 1]
-        along_y = jnp.where(not_first, pltpu.roll(centre, 1, 2), 0.0) + jnp.where(
-            not_last, pltpu.roll(centre, lanes - 1, 2), 0.0
-        )
-        if weight_z == weight_x == weight_y:
-            around = weight_z * (6.0 * centre - (along_z + along_x + along_y))
-        else:
-            around = (2.0 * (weight_z + weight_x + weight_y)) * centre - (
-                weight_z * along_z + weight_x * along_x + weight_y * along_y
+    later = {count: time % count > 0 for count in (peers, peers // 2, peers // 4)}
+
+    def pick(value, index):
+        return jnp.take_along_axis(value, index, axis=0, mode="promise_in_bounds")
+
+    def prior(value, steps):
+        return jnp.where(later[steps], pltpu.roll(value, 1, 0), 0.0)
+
+    def spread(ref, z, x, pad):
+        near = PAD2 if pad == PAD2 else NEAR
+        return jnp.broadcast_to(ref[z, pl.ds(x - pad + near, 1), :], (peers, lanes))
+
+    def around(ref, z, xs, weight_y):
+        wanted = sorted({x + step for x in xs for step in (-1, 0, 1)})
+        row = {x: ref[z, x] for x in wanted}
+        for x in xs:
+            centre = row[x]
+            across = (ref[z - 1, x] + ref[z + 1, x]) + (row[x - 1] + row[x + 1])
+            along = jnp.where(not_first, pltpu.roll(centre, 1, 1), 0.0) + jnp.where(
+                not_last, pltpu.roll(centre, lanes - 1, 1), 0.0
             )
-        left = right[z, at] + prior(centre, shift) - centre - conductivity[z, at] * around
-        return centre, left
-
-    def sweeper(new, old, right, conductivity, gain, weights, shift, base=None):
-        def work(z, x0, x1):
-            centre, left = residual(old, z, x0, x1, right, conductivity, weights, shift)
-            value = centre + gain[z, x0:x1] * left
-            new[z, x0:x1] = value if base is None else base[z, x0:x1] + value
+            total = across + along if weight_y == 1.0 else across + weight_y * along
+            yield x, centre, total
+
+    def sweeper(new, old, first, gain, hold, steps, weight_y=1.0):
+        pad = size_of(new)[0]
+
+        def work(z, xs):
+            for x, centre, total in around(old, z, xs, weight_y):
+                if first is None:
+                    value = (2.0 - OMEGA) * centre
+                else:
+                    value = (1.0 - OMEGA) * centre + first[z, x]
+                value = value + spread(gain, z, x, pad) * prior(centre, steps)
+                new[z, x] = value + spread(hold, z, x, pad) * total
 
         return work
 
-    def starter(new, right, gain):
-        def work(z, x0, x1):
-            new[z, x0:x1] = gain[z, x0:x1] * right[z, x0:x1]
+    def starter(new, right, gain, index=None):
+        pad = size_of(new)[0]
+
+        def work(z, xs):
+            for x in xs:
+                value = right[z, x] if index is None else pick(right[z, x], index)
+                new[z, x] = spread(gain, z, x, pad) * value
 
         return work
 
-    def defecter(new, old, right, weights, shift, pairs):
-        def work(z, x0, x1):
-            left = residual(old, z, x0, x1, right, cond, weights, shift)[1]
-            new[z, x0:x1] = with_partner(left, 1) if pairs else left
+    def defecter(new, old, right, stretch, steps, paired):
+        def work(z, xs):
+            for x, centre, total in around(old, z, xs, 1.0):
+                value = spread(cond, z - PAD + NEAR, x, PAD)
+                if stretch != 1.0:
+                    value = stretch * value
+                left = (right[z, x] + prior(centre, steps)) - centre
+                left = left - value * (2.0 * sum(FINE) * centre - total)
+                if paired:
+                    left = pick(left, evens) + pick(left, evens + 1)
+                new[z, x] = left
 
         return work
 
-    def wide(ref, depth, corner, stage):
+    half = peers // 2
+    of_half, of_quarter = time % half, time % (half // 2)
+    evens = 2 * of_half
+
+    def wide(ref, into, depth, corner, stage, steps):
         pad, deep, broad = size_of(ref)
 
         def spans(step, size, count):
@@ -434,14 +483,15 @@
             return pl.ds(pad, count), pl.ds(pad + size, count)
 
         out = []
-        steps = [(dz, dx) for dz in (1, -1) for dx in (1, -1)] if corner else []
-        for number, (dz, dx) in enumerate(steps + [(0, 1), (0, -1), (1, 0), (-1, 0)]):
+        corners = [(dz, dx) for dz in (1, -1) for dx in (1, -1)]
+        for number, (dz, dx) in enumerate(corners + [(0, 1), (0, -1), (1, 0), (-1, 0)]):
             count = corner if dz and dx else depth
             src_z, dst_z = spans(dz, deep, count)
             src_x, dst_x = spans(dx, broad, count)
+            some = () if steps == peers else (pl.ds(0, steps),)
             copy = pltpu.make_async_remote_copy(
-                src_ref=ref.at[src_z, src_x],
-                dst_ref=ref.at[dst_z, dst_x],
+                src_ref=ref.at[(src_z, src_x, *some)],
+                dst_ref=into.at[(dst_z, dst_x, *some)],
                 send_sem=h_send.at[stage, number],
                 recv_sem=h_recv.at[stage, number],
                 device_id=device(dz, dx),
@@ -452,19 +502,16 @@
             out.append((sends, arrives, copy))
         return out
 
-    started = []
-
-    def send(ref, depth, corner, stage):
-        copies = wide(ref, depth, corner, stage)
-        for sends, _, copy in copies:
+    started = {}
+
+    def send(ref, into, depth, corner, stage, steps):
+        started[stage] = wide(ref, into, depth, corner, stage, steps)
+        for sends, _, copy in started[stage]:
             pl.when(sends)(copy.start)
-        started.append(copies)
-
-    def receive():
-        for _, arrives, copy in started[-1]:
+
+    def receive(stage):
+        for _, arrives, copy in started[stage]:
             pl.when(arrives)(copy.wait_recv)
-
-    fine, middle, coarse = FINE, scaled(FINE, 2.0), scaled(COARSE, 4.0)
 
     def pieces_of(ref, edge):
         _, deep, broad = size_of(ref)
@@ -506,26 +553,36 @@
             outward(piece, me ^ k, me).start()
         home(piece).start()
 
-    def stages(boxes_of, works):
-        for work, (ref, rings) in zip(works, boxes_of):
-            over(strips(ref, *rings) if isinstance(rings, tuple) else (box(ref, rings),), work)
-
-    def presmooth(x, right, one, two, left, gain, weights, shift, pairs):
-        works = (
-            starter(one, right, gain),
-            sweeper(two, one, right, cond, gain, weights, shift),
-            defecter(left, two, right, weights, shift, pairs),
-        )
-        send(right, 2, 1, x)
-        stages(((one, 0), (two, -1), (left, -2)), works)
-        receive()
-        stages(((one, (2, 0)), (two, (1, -1)), (left, (0, -2))), works)
-
     own.wait()
     for k in order:
         inward(me, me ^ k, me ^ k).wait_recv()
-    presmooth(0, rhs, a1, a2, rhs1, gain0, fine, 1, True)
-    presmooth(1, rhs1, m1, m2, scrap, gain1, middle, 2, False)
+
+    send(rhs, rhs, 2, 1, 0, peers)
+    first = starter(a1, rhs, gain0)
+    second = sweeper(a2, a1, None, gain0, hold0, peers)
+    third = defecter(rhs1, a2, rhs, 1.0, peers, True)
+    over(a1, 0, None, first)
+    over(a2, -1, None, second)
+    over(rhs1, -2, None, third)
+    receive(0)
+    over(a1, 2, 0, first)
+    over(a2, 1, -1, second)
+    over(rhs1, 0, -2, third)
+
+    send(rhs1, rhs1, 2, 1, 1, half)
+    send(a2, a3, 3, 2, 2, peers)
+    first = starter(m1, rhs1, gain1, of_half)
+    second = sweeper(m2, m1, None, gain1, hold1, half)
+    third = defecter(scrap, m2, rhs1, 2.0, half, False)
+    over(m1, 0, None, first)
+    over(m2, -1, None, second)
+    over(scrap, -2, None, third)
+    receive(1)
+    over(m1, 2, 0, first)
+    over(m2, 1, -1, second)
+    over(scrap, 0, -2, third)
+
+    pairs = 2 * of_quarter
 
     def restrict(z, _):
         for x in range(half_block):
@@ -533,61 +590,76 @@
             quad = (scrap[zz, xx] + scrap[zz + 1, xx]) + (
                 scrap[zz, xx + 1] + scrap[zz + 1, xx + 1]
             )
-            rhs2[z + PAD2, x + PAD2] = 0.25 * with_partner(quad[None], 2)[0]
+            rhs2[z + PAD2, x + PAD2] = 0.25 * (pick(quad, pairs) + pick(quad, pairs + 1))
         return 0
 
     lax.fori_loop(0, half_planes, restrict, 0)
-    send(rhs2, 3, 2, 2)
-    start = starter(k1, rhs2, gain2)
-    works = [
-        sweeper(new, old, rhs2, cond2, gain2, coarse, 4)
-        for new, old in ((k2, k1), (k3, k2), (k4, k3))
-    ]
-    stages(((k1, 0), (k2, -1)), (start, works[0]))
-    receive()
-    stages(((k1, (3, 0)), (k2, (2, -1)), (k3, 1), (k4, 0)), (start, *works))
-
-    def prolong(z, x0, x1):
-        for x in range(x0, x1):
-            value = k4[z, x]
-            for dz in range(2):
-                for dx in range(2):
-                    at = (2 * (z - PAD2) + dz + PAD, 2 * (x - PAD2) + dx + PAD)
-                    m3[at] = m2[at] + value
-
-    over(strips(k4, 0, -1), prolong)
-    send(m3, 2, 1, 3)
-    over((box(k4, -1),), prolong)
-    works = (
-        sweeper(m4, m3, rhs1, cond, gain1, middle, 2),
-        sweeper(a3, m4, rhs1, cond, gain1, middle, 2, a2),
-    )
-    stages(((m4, -1), (a3, -2)), works)
-    receive()
-    stages(((m4, (1, -1)), (a3, (0, -2))), works)
-    send(a3, 2, 1, 4)
-    works = (
-        sweeper(a4, a3, rhs, cond, gain0, fine, 1),
-        sweeper(a5, a4, rhs, cond, gain0, fine, 1),
-    )
-    stages(((a4, -1), (a5, -2)), works)
+    send(rhs2, rhs2, 4, 4, 3, half // 2)
+    send(m2, m3, 2, 1, 4, half)
+    start = starter(k1, rhs2, gain2, of_quarter)
+    second, third, fourth = (
+        sweeper(new, old, first, gain2, hold2, half // 2, 4.0)
+        for new, old, first in ((k2, k1, None), (k3, k2, k1), (k4, k3, k1))
+    )
+    over(k1, 0, None, start)
+    over(k2, -1, None, second)
+    receive(3)
+    over(k1, 4, 0, start)
+    over(k2, 3, -1, second)
+    over(k3, 2, None, third)
+    over(k4, 1, None, fourth)
+
+    halved = of_half // 2
+
+    def prolonger(received):
+        def work(z, xs):
+            for x in xs:
+                value = pick(k4[z, x], halved)
+                for dz in range(2):
+                    for dx in range(2):
+                        at = (2 * (z - PAD2) + dz + PAD, 2 * (x - PAD2) + dx + PAD)
+                        base = pick(m3[at], of_half) if received else m2[at]
+                        m3[at] = base + value
+
+        return work
+
+    over(k4, 0, None, prolonger(False))
+    receive(4)
+    over(k4, 1, 0, prolonger(True))
+    over(m4, 1, None, sweeper(m4, m3, m1, gain1, hold1, half))
+    over(m5, 0, None, sweeper(m5, m4, m1, gain1, hold1, half))
+    send(m5, m5, 3, 2, 5, half)
+
+    def joiner(base):
+        def work(z, xs):
+            for x in xs:
+                a3[z, x] = base[z, x] + pick(m5[z, x], time // 2)
+
+        return work
+
+    fourth = sweeper(a4, a3, a1, gain0, hold0, peers)
+    fifth = sweeper(a5, a4, a1, gain0, hold0, peers)
+    last = defecter(fd, a5, rhs, 1.0, peers, False)
+    over(a3, 0, None, joiner(a2))
+    over(a4, -1, None, fourth)
+    over(a5, -2, None, fifth)
     ship(0)
-    receive()
-    stages(((a4, (1, -1)), (a5, (0, -2))), works)
-    send(a5, 1, 0, 5)
+    over(fd, -3, None, last)
+    receive(2)
+    receive(5)
+    over(a3, 3, 0, joiner(a3))
+    over(a4, 2, -1, fourth)
+    over(a5, 1, -2, fifth)
     for piece in range(1, 5):
         ship(piece)
-    works = (defecter(fd, a5, rhs, fine, 1, False),)
-    stages(((fd, -1),), works)
-    receive()
-    stages(((fd, (0, -1)),), works)
+    over(fd, 0, -3, last)
     ship(5)
 
-    for copies in started:
+    for copies in started.values():
         for sends, _, copy in copies:
             pl.when(sends)(copy.wait_send)
     for side, dz in ((0, 1), (1, -1)):
-        pl.when(has_z[dz])(tall_copy(side, dz).wait_send)
+        pl.when(has_z[dz])(cond_copy(side, dz).wait_send)
     for k in order:
         inward(me ^ k, me, me).wait_send()
     for piece in range(6):
@@ -604,11 +676,16 @@
     def field(depth, width):
         return pltpu.VMEM((depth, width, peers, lanes), jnp.float32)
 
+    def table(depth, width):
+        return pltpu.VMEM((depth, width, lanes), jnp.float32)
+
     large = field(planes + 2 * PAD, block + 2 * PAD)
     small = field(planes // 2 + 2 * PAD2, block // 2 + 2 * PAD2)
+    fine = table(planes + 2 * PAD, block + 2 * NEAR)
+    coarse = table(planes // 2 + 2 * PAD2, block // 2 + 2 * PAD2)
     dma = pltpu.SemaphoreType.DMA
     anywhere = pl.BlockSpec(memory_space=pl.ANY)
-    shape = jax.ShapeDtypeStruct((planes, rows, lanes), jnp.float32)
+    shape = pltpu.VMEM((planes, rows, lanes), jnp.float32)
     solution, final_defect = pl.pallas_call(
         functools.partial(cycle_kernel, peers, slabs),
         out_shape=(shape, shape),
@@ -616,19 +693,19 @@
         out_specs=(anywhere, anywhere),
         scratch_shapes=[
             large, large, small, large,
-            large, small, large, large, small,
+            table(planes + 2 * NEAR, block + 2 * NEAR),
+            fine, fine, fine, fine, coarse, coarse,
             large, large, large, large, large, large,
-            large, large, large, large,
+            large, large, large, large, large,
             small, small, small, small,
             pltpu.VMEM((planes, rows, lanes), jnp.float32),
-            pltpu.VMEM((planes + 4 * PAD2, rows, lanes), jnp.float32),
-            dma((peers,)), dma((peers,)), dma, dma((2,)),
+            dma((peers,)), dma((peers,)), dma, dma, dma((3,)),
             dma((2,)), dma((2,)),
             dma((6, 8)), dma((6, 8)),
             dma((6, peers)), dma((6, peers)), dma((6,)),
         ],
         compiler_params=pltpu.CompilerParams(
-            collective_id=0, has_side_effects=True, vmem_limit_bytes=60 * 1024 * 1024
+            collective_id=0, has_side_effects=True, vmem_limit_bytes=56 * 1024 * 1024
         ),
     )(source[0], conductivity)
     return (solution[None], final_defect[None])

time: 69.9 us -> 66.2 us (0.947)
  Pallas kernels: 66.4 us -> 63.8 us
  local copies, waits for them, and re-layouts: 2.73 us -> 1.59 us
    pallas_call x1, Pallas kernels: 66.4 us -> 63.8 us  [fused_body(): pl.pallas_call(functools.partial(cycle_kernel, peers, slabs), out_shape=(...]
    unnamed x4 -> x2, local copies, waits for them, and re-layouts: 2.73 us -> 1.59 us
where the time goes in v1:
time: 66.2 us; the launch traced here: 66 us
  Pallas kernels  63.8 us (96%)
  local copies, waits for them, and re-layouts  1.59 us (2%)
    pallas_call x1, Pallas kernels, fused_body(): pl.pallas_call(functools.partial(cycle_kernel, peers, slabs), out_shape=(...  63.8 us
    unnamed x2, local copies, waits for them, and re-layouts  1.59 us

profile of v1, /device:TPU:0, one launch (start us, length us, event | category | flops | bytes accessed | tf_op | source)
XLA Modules:
  0.0 66.0 jit_solution(5480689198631153576)
XLA Ops:
  0.6 63.8 %shard_map.41 = (f32[8,128,128]{2,1,0:T(8,128)S(1)}, f32[8,128,128]{2,1,0:T(8,128)S(1)}) custom-call(f32[8,128,128]{2,1,0:T(8,128)} %bitcast.5, f32[8,128,128]{2,1,0:T(8,128)} %conduct_far.1), custom_call_target="tpu_custom_call" | custom-call | tf_op jit(solution)/shard_map/pallas_call | solution.py:689
  64.4 0.8 %copy.6 = f32[1,8,128,128]{3,2,1,0:T(8,128)} copy(f32[1,8,128,128]{3,2,1,0:T(8,128)S(1)} %bitcast.4) | data formatting | bytes 1048576
  65.2 0.8 %copy.7 = f32[1,8,128,128]{3,2,1,0:T(8,128)} copy(f32[1,8,128,128]{3,2,1,0:T(8,128)S(1)} %bitcast.3) | data formatting | bytes 1048576

commit v2 on v1

--- a/solution.py
+++ b/solution.py
@@ -191,7 +191,7 @@
 
 PAD, PAD2 = 3, 4
 NEAR = 2 * PAD2
-UNROLL = 24
+UNROLL = 96
 
 
 def cycle_kernel(

time: 66.2 us -> 62.5 us (0.944)
  Pallas kernels: 63.8 us -> 60.1 us
    pallas_call x1, Pallas kernels: 63.8 us -> 60.1 us  [fused_body(): pl.pallas_call(functools.partial(cycle_kernel, peers, slabs), out_shape=(...]
where the time goes in v2:
time: 62.5 us; the launch traced here: 62.4 us
  Pallas kernels  60.1 us (96%)
  local copies, waits for them, and re-layouts  1.59 us (3%)
  between operations  0.64 us (1%)
    pallas_call x1, Pallas kernels, fused_body(): pl.pallas_call(functools.partial(cycle_kernel, peers, slabs), out_shape=(...  60.1 us
    unnamed x2, local copies, waits for them, and re-layouts  1.59 us

profile of v2, /device:TPU:0, one launch (start us, length us, event | category | flops | bytes accessed | tf_op | source)
XLA Modules:
  0.0 62.4 jit_solution(17402771126935518357)
XLA Ops:
  0.6 60.1 %shard_map.41 = (f32[8,128,128]{2,1,0:T(8,128)S(1)}, f32[8,128,128]{2,1,0:T(8,128)S(1)}) custom-call(f32[8,128,128]{2,1,0:T(8,128)} %bitcast.5, f32[8,128,128]{2,1,0:T(8,128)} %conduct_far.1), custom_call_target="tpu_custom_call" | custom-call | tf_op jit(solution)/shard_map/pallas_call | solution.py:689
  60.8 0.8 %copy.6 = f32[1,8,128,128]{3,2,1,0:T(8,128)} copy(f32[1,8,128,128]{3,2,1,0:T(8,128)S(1)} %bitcast.4) | data formatting | bytes 1048576
  61.6 0.8 %copy.7 = f32[1,8,128,128]{3,2,1,0:T(8,128)} copy(f32[1,8,128,128]{3,2,1,0:T(8,128)S(1)} %bitcast.3) | data formatting | bytes 1048576

commit v3 on v2

--- a/solution.py
+++ b/solution.py
@@ -206,11 +206,12 @@
     a1, a2, a3, a4, a5, fd,
     m1, m2, m3, m4, m5,
     k1, k2, k3, k4,
-    source,
-    in_send, in_recv, own_sem, load_sem, cond_load,
+    source, before, outer, conduct,
+    in_send, in_recv, own_sem, load_sem, cond_load, conduct_load,
     cond_send, cond_recv,
     h_send, h_recv,
-    out_send, out_recv, out_own,
+    late_send, early_send, pair_send, relay_send, sol_recv, before_recv,
+    sol_own, before_own, fd_send, fd_recv, fd_own, outer_send, outer_recv,
 ):
     planes, rows, lanes = source.shape
     block = rows // peers
@@ -279,6 +280,7 @@
             cond_load.at[number],
         )
 
+    load_whole = pltpu.make_async_copy(conduct_far, conduct, conduct_load)
     window(0).start()
     pl.when(has_x[-1])(window(1).start)
     pl.when(has_x[1])(window(2).start)
@@ -323,6 +325,7 @@
         own_sem,
     )
     own.start()
+    load_whole.start()
     window(0).wait()
     pl.when(has_x[-1])(window(1).wait)
     pl.when(has_x[1])(window(2).wait)
@@ -339,6 +342,12 @@
 
     for side, dz in ((0, 1), (1, -1)):
         pl.when(has_z[dz])(cond_copy(side, dz).start)
+
+    for side, dz in ((0, -1), (1, 1)):
+
+        @pl.when(jnp.logical_not(has_z[dz]))
+        def _(side=side):
+            outer[side] = jnp.zeros((rows, lanes), jnp.float32)
 
     for ref in (rhs, rhs1, a3, m3, m5, rhs2):
         pad, deep, broad = size_of(ref)
@@ -523,35 +532,110 @@
             (edge, deep - 2 * edge, broad - edge, edge),
         )
 
-    pieces = [(a5, out_solution, part) for part in pieces_of(a5, 2)]
-    pieces.append((fd, out_defect, (0, planes, 0, block)))
-
-    def ends(piece, step, owner):
-        src, dst, (z, deep, x, broad) = pieces[piece]
-        return (
-            src.at[pl.ds(z + PAD, deep), pl.ds(x + PAD, broad), step, :],
-            dst.at[pl.ds(z, deep), pl.ds(snake(owner) * block + x, broad), :],
-        )
-
-    def outward(piece, peer, owner):
-        src, dst = ends(piece, peer, owner)
+    parts = pieces_of(a5, 2)
+    pair, odd = me // 2, me % 2
+    partner = me + 1 - 2 * odd
+    others = sorted(range(1, peers // 2), reverse=True)
+
+    def on_parity(work):
+        pl.when(odd == 0)(functools.partial(work, 0))
+        pl.when(odd == 1)(functools.partial(work, 1))
+
+    def cut(step, piece):
+        z, deep, x, broad = parts[piece]
+        return a5.at[pl.ds(z + PAD, deep), pl.ds(x + PAD, broad), step, :]
+
+    def laid(ref, owner, piece):
+        z, deep, x, broad = parts[piece]
+        return ref.at[pl.ds(z, deep), pl.ds(snake(owner) * block + x, broad), :]
+
+    def place(parity):
+        return (before, before_recv) if parity else (out_solution, sol_recv)
+
+    def remote(src, dst, send_sem, recv_sem, peer):
         return pltpu.make_async_remote_copy(
             src_ref=src,
             dst_ref=dst,
-            send_sem=out_send.at[piece, peer],
-            recv_sem=out_recv.at[piece, owner],
+            send_sem=send_sem,
+            recv_sem=recv_sem,
             device_id={"tm": peer},
             device_id_type=MESH,
         )
 
-    def home(piece):
-        src, dst = ends(piece, me, me)
-        return pltpu.make_async_copy(src, dst, out_own.at[piece])
+    def late(piece, group, owner, peer):
+        return remote(
+            cut(peer, piece), laid(out_solution, owner, piece),
+            late_send.at[piece, group], sol_recv.at[piece, owner], peer,
+        )
+
+    def early(parity, piece, group, owner, step, peer):
+        into, arrived = place(parity)
+        return remote(
+            cut(step, piece), laid(into, owner, piece),
+            early_send.at[piece, group], arrived.at[piece, owner], peer,
+        )
+
+    def to_partner(parity, piece, owner):
+        into, arrived = place(1 - parity)
+        return remote(
+            cut(2 * pair, piece), laid(into, owner, piece),
+            pair_send.at[piece], arrived.at[piece, owner], partner,
+        )
+
+    def relay(parity, piece, group, owner):
+        source_of = place(parity)[0]
+        into, arrived = place(1 - parity)
+        return remote(
+            laid(source_of, owner, piece), laid(into, owner, piece),
+            relay_send.at[piece, group], arrived.at[piece, owner], partner,
+        )
+
+    def own_solution(piece):
+        return pltpu.make_async_copy(cut(me, piece), laid(out_solution, me, piece), sol_own.at[piece])
+
+    def own_before(piece):
+        return pltpu.make_async_copy(cut(me - 1, piece), laid(before, me, piece), before_own.at[piece])
 
     def ship(piece):
-        for k in order:
-            outward(piece, me ^ k, me).start()
-        home(piece).start()
+        for k in others:
+            group = pair ^ k
+            late(piece, group, me, 2 * group + 1).start()
+
+            def begin(parity, group=group):
+                early(parity, piece, group, me, 2 * group, 2 * group + parity).start()
+
+            on_parity(begin)
+
+        def near(parity):
+            to_partner(parity, piece, me).start()
+            if parity:
+                own_before(piece).start()
+            else:
+                late(piece, pair, me, partner).start()
+
+        on_parity(near)
+        own_solution(piece).start()
+
+    def fd_copy(group, owner):
+        return remote(
+            fd.at[pl.ds(PAD, planes), pl.ds(PAD, block), 2 * group, :],
+            out_defect.at[:, pl.ds(pl.multiple_of(snake(owner) * block, 8), block), :],
+            fd_send.at[group], fd_recv.at[owner], 2 * group,
+        )
+
+    own_fd = pltpu.make_async_copy(
+        fd.at[pl.ds(PAD, planes), pl.ds(PAD, block), me, :], out_defect.at[:, rows_of(me), :], fd_own
+    )
+
+    def outer_copy(side, dz):
+        return pltpu.make_async_remote_copy(
+            src_ref=out_solution.at[planes - 1 if dz > 0 else 0],
+            dst_ref=outer.at[0 if dz > 0 else 1],
+            send_sem=outer_send.at[side],
+            recv_sem=outer_recv.at[side],
+            device_id={"space": slab + dz},
+            device_id_type=MESH,
+        )
 
     own.wait()
     for k in order:
@@ -653,7 +737,69 @@
     for piece in range(1, 5):
         ship(piece)
     over(fd, 0, -3, last)
-    ship(5)
+    for k in others:
+        fd_copy(pair ^ k, me).start()
+    pl.when(odd == 0)(own_fd.start)
+    pl.when(odd == 1)(fd_copy(pair, me).start)
+
+    def forward(parity):
+        arrived_in = early
+        for piece in range(5):
+            for k in reversed(others):
+                owner = 2 * (pair ^ k) + parity
+                arrived_in(parity, piece, 0, owner, 2 * pair, me).wait_recv()
+                relay(parity, piece, pair ^ k, owner).start()
+
+    on_parity(forward)
+
+    @pl.when(odd == 1)
+    def _():
+        for piece in (1, 2, 0, 3, 4):
+            own_solution(piece).wait()
+            for k in range(1, peers):
+                late(piece, 0, me ^ k, me).wait_recv()
+            if piece in (1, 2):
+                side, dz = ((1, -1), (0, 1))[piece - 1]
+                pl.when(has_z[dz])(outer_copy(side, dz).start)
+        load_whole.wait()
+        for piece in range(5):
+            own_before(piece).wait()
+            to_partner(0, piece, partner).wait_recv()
+            for k in others:
+                relay(0, piece, 0, 2 * (pair ^ k)).wait_recv()
+        for side, dz in ((0, 1), (1, -1)):
+            pl.when(has_z[-dz])(outer_copy(side, dz).wait_recv)
+        row = lax.broadcasted_iota(jnp.int32, (rows, lanes), 0)
+        column = lax.broadcasted_iota(jnp.int32, (rows, lanes), 1)
+        for z in range(planes):
+            centre = out_solution[z]
+            across = (out_solution[z - 1] if z else outer[0]) + (
+                out_solution[z + 1] if z < planes - 1 else outer[1]
+            )
+            across = across + (
+                jnp.where(row > 0, pltpu.roll(centre, 1, 0), 0.0)
+                + jnp.where(row < rows - 1, pltpu.roll(centre, rows - 1, 0), 0.0)
+            )
+            along = jnp.where(column > 0, pltpu.roll(centre, 1, 1), 0.0) + jnp.where(
+                column < lanes - 1, pltpu.roll(centre, lanes - 1, 1), 0.0
+            )
+            left = (source[z] + before[z]) - centre
+            out_defect[z] = left - conduct[z] * (2.0 * sum(FINE) * centre - (across + along))
+        for side, dz in ((0, 1), (1, -1)):
+            pl.when(has_z[dz])(outer_copy(side, dz).wait_send)
+
+    @pl.when(odd == 0)
+    def _():
+        load_whole.wait()
+        own_fd.wait()
+        for piece in range(5):
+            own_solution(piece).wait()
+            late(piece, pair, me, partner).wait_send()
+            to_partner(1, piece, partner).wait_recv()
+            for k in others:
+                relay(1, piece, 0, 2 * (pair ^ k) + 1).wait_recv()
+        for k in range(1, peers):
+            fd_copy(pair, me ^ k).wait_recv()
 
     for copies in started.values():
         for sends, _, copy in copies:
@@ -662,11 +808,19 @@
         pl.when(has_z[dz])(cond_copy(side, dz).wait_send)
     for k in order:
         inward(me ^ k, me, me).wait_send()
-    for piece in range(6):
-        home(piece).wait()
-        for k in order:
-            outward(piece, me ^ k, me).wait_send()
-            outward(piece, me, me ^ k).wait_recv()
+    for k in others:
+        fd_copy(pair ^ k, me).wait_send()
+    pl.when(odd == 1)(fd_copy(pair, me).wait_send)
+
+    def finish(parity):
+        for piece in range(5):
+            to_partner(parity, piece, me).wait_send()
+            for k in others:
+                late(piece, pair ^ k, me, me).wait_send()
+                early(parity, piece, pair ^ k, me, 0, me).wait_send()
+                relay(parity, piece, pair ^ k, 2 * (pair ^ k) + parity).wait_send()
+
+    on_parity(finish)
 
 
 def fused_body(peers, slabs, source, conductivity):
@@ -685,12 +839,13 @@
     coarse = table(planes // 2 + 2 * PAD2, block // 2 + 2 * PAD2)
     dma = pltpu.SemaphoreType.DMA
     anywhere = pl.BlockSpec(memory_space=pl.ANY)
+    local = pl.BlockSpec(memory_space=pltpu.VMEM)
     shape = pltpu.VMEM((planes, rows, lanes), jnp.float32)
     solution, final_defect = pl.pallas_call(
         functools.partial(cycle_kernel, peers, slabs),
         out_shape=(shape, shape),
         in_specs=[anywhere, anywhere],
-        out_specs=(anywhere, anywhere),
+        out_specs=(local, local),
         scratch_shapes=[
             large, large, small, large,
             table(planes + 2 * NEAR, block + 2 * NEAR),
@@ -699,10 +854,15 @@
             large, large, large, large, large,
             small, small, small, small,
             pltpu.VMEM((planes, rows, lanes), jnp.float32),
-            dma((peers,)), dma((peers,)), dma, dma, dma((3,)),
+            pltpu.VMEM((planes, rows, lanes), jnp.float32),
+            pltpu.VMEM((2, rows, lanes), jnp.float32),
+            pltpu.VMEM((planes, rows, lanes), jnp.float32),
+            dma((peers,)), dma((peers,)), dma, dma, dma((3,)), dma,
             dma((2,)), dma((2,)),
             dma((6, 8)), dma((6, 8)),
-            dma((6, peers)), dma((6, peers)), dma((6,)),
+            dma((5, peers // 2)), dma((5, peers // 2)), dma((5,)), dma((5, peers // 2)),
+            dma((5, peers)), dma((5, peers)), dma((5,)), dma((5,)),
+            dma((peers // 2,)), dma((peers,)), dma, dma((2,)), dma((2,)),
         ],
         compiler_params=pltpu.CompilerParams(
             collective_id=0, has_side_effects=True, vmem_limit_bytes=56 * 1024 * 1024

time: 62.5 us -> 58.1 us (0.930)
  Pallas kernels: 60.1 us -> 55.7 us
    pallas_call x1, Pallas kernels: 60.1 us -> 55.7 us  [fused_body(): pl.pallas_call(functools.partial(cycle_kernel, peers, slabs), out_shape=(...]
where the time goes in v3:
time: 58.1 us; the launch traced here: 57.9 us
  Pallas kernels  55.7 us (96%)
  local copies, waits for them, and re-layouts  1.59 us (3%)
  between operations  0.64 us (1%)
    pallas_call x1, Pallas kernels, fused_body(): pl.pallas_call(functools.partial(cycle_kernel, peers, slabs), out_shape=(...  55.7 us
    unnamed x2, local copies, waits for them, and re-layouts  1.59 us

profile of v3, /device:TPU:0, one launch (start us, length us, event | category | flops | bytes accessed | tf_op | source)
XLA Modules:
  0.0 57.9 jit_solution(17360074043532408280)
XLA Ops:
  0.6 55.7 %shard_map.41 = (f32[8,128,128]{2,1,0:T(8,128)S(1)}, f32[8,128,128]{2,1,0:T(8,128)S(1)}) custom-call(f32[8,128,128]{2,1,0:T(8,128)} %bitcast.5, f32[8,128,128]{2,1,0:T(8,128)} %conduct_far.1), custom_call_target="tpu_custom_call" | custom-call | tf_op jit(solution)/shard_map/pallas_call | solution.py:844
  56.3 0.8 %copy.6 = f32[1,8,128,128]{3,2,1,0:T(8,128)} copy(f32[1,8,128,128]{3,2,1,0:T(8,128)S(1)} %bitcast.4) | data formatting | bytes 1048576
  57.1 0.8 %copy.7 = f32[1,8,128,128]{3,2,1,0:T(8,128)} copy(f32[1,8,128,128]{3,2,1,0:T(8,128)S(1)} %bitcast.3) | data formatting | bytes 1048576

commit v4 on v3

--- a/solution.py
+++ b/solution.py
@@ -189,9 +189,9 @@
     )
 
 
-PAD, PAD2 = 3, 4
+PAD, PAD2 = 4, 4
 NEAR = 2 * PAD2
-UNROLL = 96
+UNROLL = 160
 
 
 def cycle_kernel(
@@ -202,7 +202,7 @@
     out_solution,
     out_defect,
     rhs, rhs1, rhs2, scrap,
-    cond, gain0, hold0, gain1, hold1, gain2, hold2,
+    cond, inner, gain0, hold0, gain1, hold1, gain2, hold2,
     a1, a2, a3, a4, a5, fd,
     m1, m2, m3, m4, m5,
     k1, k2, k3, k4,
@@ -251,6 +251,9 @@
             parts.append((z0, i0, list(range(x0, x1))))
             parts.append((i1, z1, list(range(x0, x1))))
             parts.append((i0, i1, list(range(x0, j0)) + list(range(j1, x1))))
+        over_parts(parts, work)
+
+    def over_parts(parts, work):
         for first, last, xs in parts:
             count = last - first
             if count <= 0 or not xs:
@@ -349,7 +352,7 @@
         def _(side=side):
             outer[side] = jnp.zeros((rows, lanes), jnp.float32)
 
-    for ref in (rhs, rhs1, a3, m3, m5, rhs2):
+    for ref in (rhs, m3, m5, rhs2):
         pad, deep, broad = size_of(ref)
         for dz, first in ((-1, 0), (1, pad + deep)):
 
@@ -384,6 +387,7 @@
             value = jnp.where(ok, cond[z - PAD + NEAR, at, :], 0.0)
             fine = jnp.where(ok, OMEGA / (1.0 + value * (2.0 * sum(FINE))), 0.0)
             middle = jnp.where(ok, OMEGA / (1.0 + value * (4.0 * sum(FINE))), 0.0)
+            inner[z, at, :] = value
             gain0[z, at, :] = fine
             hold0[z, at, :] = fine * value
             gain1[z, at, :] = middle
@@ -424,7 +428,7 @@
         return jnp.where(later[steps], pltpu.roll(value, 1, 0), 0.0)
 
     def spread(ref, z, x, pad):
-        near = PAD2 if pad == PAD2 else NEAR
+        near = PAD2 if ref.shape[1] == half_block + 2 * PAD2 else NEAR
         return jnp.broadcast_to(ref[z, pl.ds(x - pad + near, 1), :], (peers, lanes))
 
     def around(ref, z, xs, weight_y):
@@ -466,7 +470,7 @@
     def defecter(new, old, right, stretch, steps, paired):
         def work(z, xs):
             for x, centre, total in around(old, z, xs, 1.0):
-                value = spread(cond, z - PAD + NEAR, x, PAD)
+                value = spread(inner, z, x, PAD)
                 if stretch != 1.0:
                     value = stretch * value
                 left = (right[z, x] + prior(centre, steps)) - centre
@@ -481,22 +485,25 @@
     of_half, of_quarter = time % half, time % (half // 2)
     evens = 2 * of_half
 
-    def wide(ref, into, depth, corner, stage, steps):
+    def wide(ref, into, layers, corner_layers, stage, steps):
         pad, deep, broad = size_of(ref)
 
-        def spans(step, size, count):
+        def spans(step, size, span):
+            low, high = span
             if step == 0:
                 return pl.ds(pad, size), pl.ds(pad, size)
             if step > 0:
-                return pl.ds(pad + size - count, count), pl.ds(pad - count, count)
-            return pl.ds(pad, count), pl.ds(pad + size, count)
-
+                return pl.ds(pad + size - high, high - low), pl.ds(pad - high, high - low)
+            return pl.ds(pad + low, high - low), pl.ds(pad + size + low, high - low)
+
+        blocks = [
+            (dz, dx, *ranges) for ranges in corner_layers for dz in (1, -1) for dx in (1, -1)
+        ]
+        blocks += [(dz, dx, layers, layers) for dz, dx in ((0, 1), (0, -1), (1, 0), (-1, 0))]
         out = []
-        corners = [(dz, dx) for dz in (1, -1) for dx in (1, -1)]
-        for number, (dz, dx) in enumerate(corners + [(0, 1), (0, -1), (1, 0), (-1, 0)]):
-            count = corner if dz and dx else depth
-            src_z, dst_z = spans(dz, deep, count)
-            src_x, dst_x = spans(dx, broad, count)
+        for number, (dz, dx, z_span, x_span) in enumerate(blocks):
+            src_z, dst_z = spans(dz, deep, z_span)
+            src_x, dst_x = spans(dx, broad, x_span)
             some = () if steps == peers else (pl.ds(0, steps),)
             copy = pltpu.make_async_remote_copy(
                 src_ref=ref.at[(src_z, src_x, *some)],
@@ -513,10 +520,13 @@
 
     started = {}
 
-    def send(ref, into, depth, corner, stage, steps):
-        started[stage] = wide(ref, into, depth, corner, stage, steps)
+    def send(ref, into, layers, corner_layers, stage, steps):
+        started[stage] = wide(ref, into, layers, corner_layers, stage, steps)
         for sends, _, copy in started[stage]:
             pl.when(sends)(copy.start)
+
+    def square(depth):
+        return (((0, depth), (0, depth)),)
 
     def receive(stage):
         for _, arrives, copy in started[stage]:
@@ -641,7 +651,8 @@
     for k in order:
         inward(me, me ^ k, me ^ k).wait_recv()
 
-    send(rhs, rhs, 2, 1, 0, peers)
+    send(rhs, rhs, (0, 2), square(1), 0, peers)
+    send(rhs, rhs, (2, 4), (((0, 1), (1, 3)), ((1, 3), (0, 2))), 1, peers)
     first = starter(a1, rhs, gain0)
     second = sweeper(a2, a1, None, gain0, hold0, peers)
     third = defecter(rhs1, a2, rhs, 1.0, peers, True)
@@ -649,22 +660,39 @@
     over(a2, -1, None, second)
     over(rhs1, -2, None, third)
     receive(0)
-    over(a1, 2, 0, first)
-    over(a2, 1, -1, second)
+    top, left = PAD + planes, PAD + block
+    inside = list(range(PAD, left))
+    flank = [PAD - 2, PAD - 1, left, left + 1]
+    over_parts(
+        [(PAD - 2, PAD, inside), (top, top + 2, inside), (PAD, top, flank)]
+        + [(z, z + 1, [PAD - 1, left]) for z in (PAD - 1, top)],
+        first,
+    )
+    middle_rows = [PAD - 1, *inside, left]
+    over_parts(
+        [(PAD - 1, PAD, inside), (PAD, PAD + 1, middle_rows)]
+        + [(top - 1, top, middle_rows), (top, top + 1, inside)]
+        + [(PAD + 1, top - 1, [PAD - 1, PAD, left - 1, left])],
+        second,
+    )
     over(rhs1, 0, -2, third)
-
-    send(rhs1, rhs1, 2, 1, 1, half)
-    send(a2, a3, 3, 2, 2, peers)
-    first = starter(m1, rhs1, gain1, of_half)
-    second = sweeper(m2, m1, None, gain1, hold1, half)
-    third = defecter(scrap, m2, rhs1, 2.0, half, False)
-    over(m1, 0, None, first)
-    over(m2, -1, None, second)
-    over(scrap, -2, None, third)
+    fourth = starter(m1, rhs1, gain1)
+    fifth = sweeper(m2, m1, None, gain1, hold1, half)
+    sixth = defecter(scrap, m2, rhs1, 2.0, half, False)
+    over(m1, 0, None, fourth)
+    over(m2, -1, None, fifth)
+    over(scrap, -2, None, sixth)
     receive(1)
-    over(m1, 2, 0, first)
-    over(m2, 1, -1, second)
-    over(scrap, 0, -2, third)
+    for z in (PAD - 2, PAD - 1, top, top + 1):
+        first(z, flank)
+    over(a1, 4, 2, first)
+    for z in (PAD - 1, top):
+        second(z, [PAD - 1, left])
+    over(a2, 3, 1, second)
+    over(rhs1, 2, 0, third)
+    over(m1, 2, 0, fourth)
+    over(m2, 1, -1, fifth)
+    over(scrap, 0, -2, sixth)
 
     pairs = 2 * of_quarter
 
@@ -678,8 +706,8 @@
         return 0
 
     lax.fori_loop(0, half_planes, restrict, 0)
-    send(rhs2, rhs2, 4, 4, 3, half // 2)
-    send(m2, m3, 2, 1, 4, half)
+    send(rhs2, rhs2, (0, 4), square(4), 3, half // 2)
+    send(m2, m3, (0, 2), square(1), 4, half)
     start = starter(k1, rhs2, gain2, of_quarter)
     second, third, fourth = (
         sweeper(new, old, first, gain2, hold2, half // 2, 4.0)
@@ -712,7 +740,7 @@
     over(k4, 1, 0, prolonger(True))
     over(m4, 1, None, sweeper(m4, m3, m1, gain1, hold1, half))
     over(m5, 0, None, sweeper(m5, m4, m1, gain1, hold1, half))
-    send(m5, m5, 3, 2, 5, half)
+    send(m5, m5, (0, 3), square(2), 5, half)
 
     def joiner(base):
         def work(z, xs):
@@ -729,9 +757,8 @@
     over(a5, -2, None, fifth)
     ship(0)
     over(fd, -3, None, last)
-    receive(2)
     receive(5)
-    over(a3, 3, 0, joiner(a3))
+    over(a3, 3, 0, joiner(a2))
     over(a4, 2, -1, fourth)
     over(a5, 1, -2, fifth)
     for piece in range(1, 5):
@@ -743,35 +770,36 @@
     pl.when(odd == 1)(fd_copy(pair, me).start)
 
     def forward(parity):
-        arrived_in = early
-        for piece in range(5):
+        for piece in (0, 1, 2, None, 3, 4):
+            if piece is None:
+                if parity:
+                    for edge, side, dz in ((1, 1, -1), (2, 0, 1)):
+                        own_solution(edge).wait()
+                        for k in range(1, peers):
+                            late(edge, 0, me ^ k, me).wait_recv()
+                        pl.when(has_z[dz])(outer_copy(side, dz).start)
+                continue
             for k in reversed(others):
                 owner = 2 * (pair ^ k) + parity
-                arrived_in(parity, piece, 0, owner, 2 * pair, me).wait_recv()
+                early(parity, piece, 0, owner, 2 * pair, me).wait_recv()
                 relay(parity, piece, pair ^ k, owner).start()
 
     on_parity(forward)
 
     @pl.when(odd == 1)
     def _():
-        for piece in (1, 2, 0, 3, 4):
+        for piece in (0, 3, 4):
             own_solution(piece).wait()
             for k in range(1, peers):
                 late(piece, 0, me ^ k, me).wait_recv()
-            if piece in (1, 2):
-                side, dz = ((1, -1), (0, 1))[piece - 1]
-                pl.when(has_z[dz])(outer_copy(side, dz).start)
         load_whole.wait()
-        for piece in range(5):
-            own_before(piece).wait()
-            to_partner(0, piece, partner).wait_recv()
-            for k in others:
-                relay(0, piece, 0, 2 * (pair ^ k)).wait_recv()
-        for side, dz in ((0, 1), (1, -1)):
-            pl.when(has_z[-dz])(outer_copy(side, dz).wait_recv)
         row = lax.broadcasted_iota(jnp.int32, (rows, lanes), 0)
         column = lax.broadcasted_iota(jnp.int32, (rows, lanes), 1)
-        for z in range(planes):
+        for z in (*range(1, planes - 1), None, 0, planes - 1):
+            if z is None:
+                for side, dz in ((0, 1), (1, -1)):
+                    pl.when(has_z[-dz])(outer_copy(side, dz).wait_recv)
+                continue
             centre = out_solution[z]
             across = (out_solution[z - 1] if z else outer[0]) + (
                 out_solution[z + 1] if z < planes - 1 else outer[1]
@@ -783,8 +811,15 @@
             along = jnp.where(column > 0, pltpu.roll(centre, 1, 1), 0.0) + jnp.where(
                 column < lanes - 1, pltpu.roll(centre, lanes - 1, 1), 0.0
             )
-            left = (source[z] + before[z]) - centre
+            left = source[z] - centre
             out_defect[z] = left - conduct[z] * (2.0 * sum(FINE) * centre - (across + along))
+        for piece in range(5):
+            own_before(piece).wait()
+            to_partner(0, piece, partner).wait_recv()
+            for k in others:
+                relay(0, piece, 0, 2 * (pair ^ k)).wait_recv()
+        for z in range(planes):
+            out_defect[z] = out_defect[z] + before[z]
         for side, dz in ((0, 1), (1, -1)):
             pl.when(has_z[dz])(outer_copy(side, dz).wait_send)
 
@@ -849,7 +884,7 @@
         scratch_shapes=[
             large, large, small, large,
             table(planes + 2 * NEAR, block + 2 * NEAR),
-            fine, fine, fine, fine, coarse, coarse,
+            fine, fine, fine, fine, fine, coarse, coarse,
             large, large, large, large, large, large,
             large, large, large, large, large,
             small, small, small, small,
@@ -859,7 +894,7 @@
             pltpu.VMEM((planes, rows, lanes), jnp.float32),
             dma((peers,)), dma((peers,)), dma, dma, dma((3,)), dma,
             dma((2,)), dma((2,)),
-            dma((6, 8)), dma((6, 8)),
+            dma((6, 12)), dma((6, 12)),
             dma((5, peers // 2)), dma((5, peers // 2)), dma((5,)), dma((5, peers // 2)),
             dma((5, peers)), dma((5, peers)), dma((5,)), dma((5,)),
             dma((peers // 2,)), dma((peers,)), dma, dma((2,)), dma((2,)),

time: 58.1 us -> 56.9 us (0.979)
  Pallas kernels: 55.7 us -> 54.6 us
    pallas_call x1, Pallas kernels: 55.7 us -> 54.6 us  [fused_body(): pl.pallas_call(functools.partial(cycle_kernel, peers, slabs), out_shape=(...]
where the time goes in v4:
time: 56.9 us; the launch traced here: 56.8 us
  Pallas kernels  54.6 us (96%)
  local copies, waits for them, and re-layouts  1.59 us (3%)
  between operations  0.64 us (1%)
    pallas_call x1, Pallas kernels, fused_body(): pl.pallas_call(functools.partial(cycle_kernel, peers, slabs), out_shape=(...  54.6 us
    unnamed x2, local copies, waits for them, and re-layouts  1.59 us

profile of v4, /device:TPU:0, one launch (start us, length us, event | category | flops | bytes accessed | tf_op | source)
XLA Modules:
  0.0 56.8 jit_solution(13647385114054756802)
XLA Ops:
  0.6 54.6 %shard_map.41 = (f32[8,128,128]{2,1,0:T(8,128)S(1)}, f32[8,128,128]{2,1,0:T(8,128)S(1)}) custom-call(f32[8,128,128]{2,1,0:T(8,128)} %bitcast.5, f32[8,128,128]{2,1,0:T(8,128)} %conduct_far.1), custom_call_target="tpu_custom_call" | custom-call | tf_op jit(solution)/shard_map/pallas_call | solution.py:879
  55.2 0.8 %copy.6 = f32[1,8,128,128]{3,2,1,0:T(8,128)} copy(f32[1,8,128,128]{3,2,1,0:T(8,128)S(1)} %bitcast.4) | data formatting | bytes 1048576
  56.0 0.8 %copy.7 = f32[1,8,128,128]{3,2,1,0:T(8,128)} copy(f32[1,8,128,128]{3,2,1,0:T(8,128)S(1)} %bitcast.3) | data formatting | bytes 1048576
